TPU v7x, 128 devices: a whole 4x4x4 slice. The times are simulated.
128 devices in a mesh: ep: 32 (over z, x, core), dp: 4 (over y).
Axes of the slice: x: 4, y: 4, z: 4, core: 2. Of those that a mesh axis runs over, the one named last changes fastest.
Arguments:
- grad_out: float32 [16384, 1536], P(('ep', 'dp')), may hold values from -6 to 6
- tokens: bfloat16 [16384, 1536], P(('ep', 'dp')), may hold values from -6 to 6
- probs: float32 [16384, 4], P(('ep', 'dp')), may hold values from 0.1 to 0.5
- expert_ids: int32 [16384, 4], P(('ep', 'dp')), may hold values from 0 to 31, all different within a row; in each aligned block of 128 rows (0 to 127, 128 to 255, ...) at most 20 rows name the same one
- priority: int32 [128, 128], P(('ep', 'dp')), may hold values from 0 to 127, each once within a row
- cap_counts: int32 [32], replicated, may hold values from 10 to 20, as said below
- gate_weight: bfloat16 [32, 1536, 1536], P('ep'), may hold values from -0.15625 to 0.15625
- up_weight: bfloat16 [32, 1536, 1536], P('ep'), may hold values from -0.15625 to 0.15625
- down_weight: bfloat16 [32, 1536, 1536], P('ep'), may hold values from -0.15625 to 0.15625
Outputs:
- input_grad: bfloat16 [16384, 1536], P(('ep', 'dp'))
- prob_grad: float32 [16384, 4], P(('ep', 'dp'))
- gate_grad: bfloat16 [32, 1536, 1536], P('ep', 'dp')
- up_grad: bfloat16 [32, 1536, 1536], P('ep', 'dp')
- down_grad: bfloat16 [32, 1536, 1536], P('ep', 'dp')
Inputs may be any that keep to these rules, and one draw needn't show every extreme that they name: `expert_ids`: each row names 4 different experts; among the rows of one device no expert is named by more than 20 rows, and in some device some expert is named by exactly 20 rows. `priority`: each row orders the 128 tokens of one device, each number once. `cap_counts`: some expert has exactly 20.
All inputs are finite; a program needn't handle non-finite values. Where the computation divides by a largest or mean magnitude, that divisor is 1e-20 or more.
Results may differ from a plain program's by a relative error of at most 0.017.
Values may be sent and summed in bfloat16 or wider, within the bound.
A program may use at most 128 MiB of HBM per device.

v0:
```python
import jax
import jax.numpy as jnp
from jax import lax
from jax.sharding import PartitionSpec as P

sharpness = 1.702


def contract_last(first_op, second_op):
    return lax.dot_general(
        first_op, second_op, (((1,), (1,)), ((), ())), preferred_element_type=jnp.float32
    )


def contract_first(first_op, second_op):
    return lax.dot_general(
        first_op, second_op, (((0,), (0,)), ((), ())), preferred_element_type=jnp.float32
    )


def route_table(expert_ids, priority, cap_counts, buckets, capacity):
    ranking = priority[0]
    earlier = (ranking[None, :] < ranking[:, None]).astype(jnp.float32)
    expert_range = lax.broadcasted_iota(jnp.int32, (1, 1, buckets), 2)
    matches = (expert_ids[:, :, None] == expert_range).astype(jnp.float32)
    routed = jnp.sum(matches, axis=1)
    before = jnp.dot(earlier, routed)
    slot_rank = jnp.sum(matches * before[:, None, :], axis=2)
    keep_limit = jnp.sum(matches * cap_counts.astype(jnp.float32)[None, None, :], axis=2)
    slot_range = lax.broadcasted_iota(jnp.float32, (1, 1, capacity), 2)
    slot_hit = (
        (slot_rank[:, :, None] == slot_range) & (slot_rank < keep_limit)[:, :, None]
    ).astype(jnp.float32)
    placement = matches[:, :, :, None] * slot_hit[:, :, None, :]
    return placement.reshape(expert_ids.shape[0], expert_ids.shape[1], buckets * capacity)


def deltas(slot_x, slot_g, w_gate, w_up, w_down):
    gate_pre = contract_last(slot_x, w_gate)
    up_pre = contract_last(slot_x, w_up)
    act_delta = contract_last(slot_g, w_down)
    squash = jax.nn.sigmoid(sharpness * gate_pre)
    gated = gate_pre * squash
    activated = (up_pre + 1.0) * gated
    up_delta = (act_delta * gated).astype(jnp.bfloat16)
    gate_delta = (
        act_delta * (up_pre + 1.0) * (squash + sharpness * gate_pre * squash * (1.0 - squash))
    ).astype(jnp.bfloat16)
    return (activated, act_delta, gate_delta, up_delta)


def on_device(
    grad_out, tokens, probs, expert_ids, priority, cap_counts, gate_weight, up_weight, down_weight
):
    ep_size = lax.axis_size("ep")
    dp_size = lax.axis_size("dp")
    tok_rows, model_width = tokens.shape
    route_count = expert_ids.shape[1]
    capacity = 5 * route_count * tok_rows // (4 * ep_size)
    slot_rows = ep_size * capacity
    placement = route_table(expert_ids, priority, cap_counts, ep_size, capacity)
    slot_table = jnp.sum(placement, axis=1)
    table_low = slot_table.astype(jnp.bfloat16)
    row_scale = jnp.maximum(jnp.max(jnp.abs(grad_out), axis=1), 1.0)
    quantized = (grad_out / row_scale[:, None]).astype(jnp.bfloat16)
    send_prob = jnp.sum(placement * probs[:, :, None], axis=(0, 1))
    send_scale = jnp.sum(slot_table * row_scale[:, None], axis=0)
    send_x = jnp.einsum("ts,td->sd", table_low, tokens, preferred_element_type=jnp.float32).astype(
        jnp.bfloat16
    )
    send_g = (
        jnp.einsum("ts,td->sd", table_low, quantized, preferred_element_type=jnp.float32)
        * (send_prob * send_scale)[:, None]
    ).astype(jnp.bfloat16)
    bucket_shape = (ep_size, capacity, model_width)

    def exchange(a):
        return lax.all_to_all(a, "ep", split_axis=0, concat_axis=0, tiled=True)

    slot_x = exchange(send_x.reshape(bucket_shape)).reshape(slot_rows, model_width)
    all_x = lax.all_gather(slot_x, "dp", axis=0, tiled=True)
    slot_g = exchange(send_g.reshape(bucket_shape)).reshape(slot_rows, model_width)
    all_g = lax.all_gather(slot_g, "dp", axis=0, tiled=True)
    w_gate = gate_weight[0]
    w_up = up_weight[0]
    w_down = down_weight[0]
    activated, act_delta, gate_delta, up_delta = deltas(slot_x, slot_g, w_gate, w_up, w_down)
    slot_in = (
        jnp.dot(gate_delta, w_gate, preferred_element_type=jnp.float32)
        + jnp.dot(up_delta, w_up, preferred_element_type=jnp.float32)
    ).astype(jnp.bfloat16)
    slot_out = jnp.sum(activated * act_delta, axis=1)
    back_in = exchange(slot_in.reshape(bucket_shape))
    back_prob = exchange(slot_out.reshape(ep_size, capacity).astype(jnp.bfloat16))
    prob_grad = jnp.einsum("tks,s->tk", placement, back_prob.reshape(slot_rows)) / probs
    input_grad = jnp.einsum(
        "ts,sd->td",
        table_low,
        back_in.reshape(slot_rows, model_width),
        preferred_element_type=jnp.float32,
    ).astype(jnp.bfloat16)
    share = w_gate.shape[0] // dp_size
    first = lax.axis_index("dp") * share

    def mine(w):
        return lax.dynamic_slice_in_dim(w, first, share, 0)

    act_mine, _, gd_mine, ud_mine = deltas(all_x, all_g, mine(w_gate), mine(w_up), mine(w_down))
    gate_share = contract_first(gd_mine, all_x).astype(jnp.bfloat16)
    up_share = contract_first(ud_mine, all_x).astype(jnp.bfloat16)
    down_share = contract_first(act_mine.astype(jnp.bfloat16), all_g).astype(jnp.bfloat16)
    return (input_grad, prob_grad, gate_share[None], up_share[None], down_share[None])


def solution(mesh):
    return jax.shard_map(
        on_device,
        mesh=mesh,
        in_specs=(
            P(("ep", "dp"), None),
            P(("ep", "dp"), None),
            P(("ep", "dp"), None),
            P(("ep", "dp"), None),
            P(("ep", "dp"), None),
            P(),
            P("ep", None, None),
            P("ep", None, None),
            P("ep", None, None),
        ),
        out_specs=(
            P(("ep", "dp"), None),
            P(("ep", "dp"), None),
            P("ep", "dp", None),
            P("ep", "dp", None),
            P("ep", "dp", None),
        ),
        check_vma=False,
    )
```

profile of v0, /device:TPU:1, one launch (start us, length us, event | category | flops | bytes accessed | tf_op | source)
XLA Modules:
  0.0 248.0 jit_solution(7221112332950681031)
XLA Ops:
  7.2 0.0 copy-start
  7.2 0.0 all-gather.5.cloned.1.call-start
  7.2 0.7 convert_element_type.78
  7.9 0.7 fusion.39
  8.6 0.8 select_reduce_fusion
  9.4 0.9 fusion.40
  10.3 0.7 select_reduce_fusion.1
  11.1 1.3 abs_reduce_fusion
  12.4 1.0 fusion.24
  13.3 0.2 multiply_reduce_fusion.2
  13.5 0.1 copy.29
  13.6 1.9 convolution_convert_fusion
  15.6 2.5 reshape.94
  18.0 40.7 %all_to_all.24 = bf16[32,20,1536]{2,1,0:T(8,128)(2,1)} all-to-all(bf16[32,20,1536]{2,1,0:T(8,128)(2,1)S(1)} %reshape.94), channel_id=1, replica_groups=mesh['ep'=32,'dp'=4] {'ep'}, dimensions={0} | all-to-all | bytes 3932160 | tf_op jit(solution)/shard_map/all_to_all | solution.py:78
  58.7 4.1 %reshape.95 = bf16[640,1536]{1,0:T(8,128)(2,1)} reshape(bf16[32,20,1536]{2,1,0:T(8,128)(2,1)} %all_to_all.24) | data formatting | bytes 3932160 | tf_op jit(solution)/shard_map/reshape | solution.py:80
  62.8 0.0 all-gather.5.cloned.1.call-update
  62.8 0.0 all-gather.3.cloned.1.call-start
  62.9 0.1 copy.30
  62.9 0.1 mul.136
  63.1 2.1 multiply_convert_fusion.5
  65.2 2.5 reshape.92
  67.6 35.0 %all_to_all.25 = bf16[32,20,1536]{2,1,0:T(8,128)(2,1)} all-to-all(bf16[32,20,1536]{2,1,0:T(8,128)(2,1)S(1)} %reshape.92), channel_id=1, replica_groups=mesh['ep'=32,'dp'=4] {'ep'}, dimensions={0} | all-to-all | bytes 3932160 | tf_op jit(solution)/shard_map/all_to_all | solution.py:78
  102.6 4.1 %reshape.93 = bf16[640,1536]{1,0:T(8,128)(2,1)} reshape(bf16[32,20,1536]{2,1,0:T(8,128)(2,1)} %all_to_all.25) | data formatting | bytes 3932160 | tf_op jit(solution)/shard_map/reshape | solution.py:82
  106.8 0.0 all-gather.3.cloned.1.call-update
  106.8 0.0 slice-start.2
  106.8 5.3 %fusion.6 = f32[640,1536]{1,0:T(8,128)S(1)} fusion(bf16[640,1536]{1,0:T(8,128)(2,1)S(1)} %copy-done.2, bf16[1,1536,1536]{2,1,0:T(8,128)(2,1)} %param.16), kind=kOutput, calls=%fused_computation.6 | convolution fusion | flops 3019898880 | bytes 10616832 | tf_op jit(solution)/shard_map/dot_general | solution.py:10
  112.1 0.0 slice-start.3
  112.1 6.6 %fusion.2 = f32[640,1536]{1,0:T(8,128)S(1)} fusion(bf16[640,1536]{1,0:T(8,128)(2,1)S(1)} %copy-done.2, bf16[1,1536,1536]{2,1,0:T(8,128)(2,1)} %param.15), kind=kOutput, calls=%fused_computation.2 | convolution fusion | flops 3019898880 | bytes 10616832 | tf_op jit(solution)/shard_map/dot_general | solution.py:10
  118.8 5.4 %multiply_reduce_fusion = (bf16[640]{0:T(1024)(128)(2,1)S(1)}, f32[640,1536]{1,0:T(8,128)}) fusion(f32[640,1536]{1,0:T(8,128)S(1)} %fusion.6, f32[640,1536]{1,0:T(8,128)S(1)} %fusion.2, bf16[640,1536]{1,0:T(8,128)(2,1)S(1)} %copy-done.3, bf16[1,1536,1536]{2,1,0:T(8,128)(2,1)S(1)} %bitcast.64), kind=kOutput, calls=%fused_computation.15 | convolution fusion | flops 3028745728 | bytes 18482432 | tf_op jit(solution)/shard_map/dot_general | solution.py:10
  124.2 0.7 convert_element_type.97
  124.9 3.8 %all-to-all-start.3 = ((bf16[32,1,20]{2,1,0:T(2,128)(2,1)}), bf16[32,1,20]{2,1,0:T(2,128)(2,1)S(1)}, u32[]{:S(2)}, u32[]{:S(2)}) async-start(bf16[32,1,20]{2,1,0:T(2,128)(2,1)} %convert_element_type.97), calls=%async_computation.3 | async-start | bytes 32768 | tf_op jit(solution)/shard_map/all_to_all | solution.py:78
  128.8 8.9 %fusion = f32[640,1536]{1,0:T(8,128)S(1)} fusion(bf16[1,1536,1536]{2,1,0:T(8,128)(2,1)} %param.15, f32[640,1536]{1,0:T(8,128)} %get-tuple-element.12, f32[640,1536]{1,0:T(8,128)} %copy-done.9, f32[640,1536]{1,0:T(8,128)} %copy-done.11), kind=kOutput, calls=%fused_computation | convolution fusion | flops 3031695360 | bytes 20447232 | tf_op jit(solution)/shard_map/dot_general | solution.py:89
  137.7 5.8 %add_convert_fusion = bf16[640,1536]{1,0:T(8,128)(2,1)S(1)} fusion(f32[640,1536]{1,0:T(8,128)S(1)} %fusion, bf16[1,1536,1536]{2,1,0:T(8,128)(2,1)} %param.16, f32[640,1536]{1,0:T(8,128)S(1)} %copy-done.13, f32[640,1536]{1,0:T(8,128)S(1)} %copy-done.10), kind=kOutput, calls=%fused_computation.16 | convolution fusion | flops 3028746240 | bytes 18481152 | tf_op jit(solution)/shard_map/dot_general | solution.py:90
  143.6 0.0 copy-start.5
  143.6 2.1 reshape.96
  145.7 7.3 %all-to-all-start.2 = ((bf16[32,20,1536]{2,1,0:T(8,128)(2,1)}), bf16[32,20,1536]{2,1,0:T(8,128)(2,1)S(1)}, u32[]{:S(2)}, u32[]{:S(2)}) async-start(bf16[32,20,1536]{2,1,0:T(8,128)(2,1)} %reshape.96), calls=%async_computation.2 | async-start | bytes 4718592 | tf_op jit(solution)/shard_map/all_to_all | solution.py:78
  153.0 0.1 copy.33
  153.1 0.2 fusion.17
  153.4 0.6 div.20
  154.0 30.6 %all-to-all-done.2 = bf16[32,20,1536]{2,1,0:T(8,128)(2,1)S(1)} async-done(((bf16[32,20,1536]{2,1,0:T(8,128)(2,1)}), bf16[32,20,1536]{2,1,0:T(8,128)(2,1)S(1)}, u32[]{:S(2)}, u32[]{:S(2)}) %all-to-all-start.2) | async-done | bytes 1966112 | tf_op jit(solution)/shard_map/all_to_all | solution.py:78
  184.5 1.5 fusion.19
  186.1 9.9 %fusion.25 = f32[2560,384]{1,0:T(8,128)} fusion(bf16[2560,1536]{1,0:T(8,128)(2,1)} %all-gather.5.cloned.1.call-done, bf16[1,1536,1536]{2,1,0:T(8,128)(2,1)} %param.15, s32[]{:T(128)S(6)} %select_n.2), kind=kOutput, calls=%fused_computation.41 | convolution fusion | flops 3019898880 | bytes 12976132 | tf_op jit(solution)/shard_map/dot_general | solution.py:10
  196.0 7.5 %convolution_add_fusion = f32[2560,384]{1,0:T(8,128)} fusion(bf16[2560,1536]{1,0:T(8,128)(2,1)S(1)} %copy-done.6, bf16[1,1536,1536]{2,1,0:T(8,128)(2,1)} %param.16, s32[]{:T(128)S(6)} %select_n.2), kind=kOutput, calls=%fused_computation.10 | convolution fusion | flops 3020881920 | bytes 12976132 | tf_op jit(solution)/shard_map/dot_general | solution.py:10
  203.4 16.9 %all-gather.3.cloned.1.call-done = bf16[2560,1536]{1,0:T(8,128)(2,1)} async-done(((bf16[640,1536]{1,0:T(8,128)(2,1)}), bf16[2560,1536]{1,0:T(8,128)(2,1)}) %all-gather.3.cloned.1.call-update) | async-done | bytes 7864336 | tf_op jit(solution)/shard_map/all_gather | solution.py:83
  220.3 7.4 %fusion.28 = f32[2560,384]{1,0:T(8,128)S(1)} fusion(bf16[2560,1536]{1,0:T(8,128)(2,1)} %all-gather.3.cloned.1.call-done, bf16[1,1536,1536]{2,1,0:T(8,128)(2,1)} %param.17, s32[]{:T(128)S(6)} %select_n.2), kind=kOutput, calls=%fused_computation.44 | convolution fusion | flops 3019898880 | bytes 12976132 | tf_op jit(solution)/shard_map/dot_general | solution.py:10
  227.7 4.4 %fusion.15 = bf16[1,384,1536]{2,1,0:T(8,128)(2,1)} fusion(bf16[2560,1536]{1,0:T(8,128)(2,1)S(1)} %copy-done.7, f32[2560,384]{1,0:T(8,128)S(1)} %fusion.28, f32[2560,384]{1,0:T(8,128)S(1)} %copy-done.8), kind=kOutput, calls=%fused_computation.28 | convolution fusion | flops 3027369984 | bytes 16908288 | tf_op jit(solution)/shard_map/dot_general | solution.py:16
  232.2 4.5 %fusion.14 = bf16[1,384,1536]{2,1,0:T(8,128)(2,1)} fusion(bf16[2560,1536]{1,0:T(8,128)(2,1)S(1)} %copy-done.7, f32[2560,384]{1,0:T(8,128)S(1)} %fusion.28, f32[2560,384]{1,0:T(8,128)S(1)} %copy-done.12, f32[2560,384]{1,0:T(8,128)S(1)} %copy-done.8), kind=kOutput, calls=%fused_computation.27 | convolution fusion | flops 3031302144 | bytes 20840448 | tf_op jit(solution)/shard_map/dot_general | solution.py:16
  236.7 4.4 %fusion.16 = bf16[1,384,1536]{2,1,0:T(8,128)(2,1)} fusion(bf16[2560,1536]{1,0:T(8,128)(2,1)S(1)} %bitcast.62, f32[2560,384]{1,0:T(8,128)S(1)} %copy-done.12, f32[2560,384]{1,0:T(8,128)S(1)} %copy-done.8), kind=kOutput, calls=%fused_computation.29 | convolution fusion | flops 3027369984 | bytes 16908288 | tf_op jit(solution)/shard_map/dot_general | solution.py:16
  (41 shorter events, 0.1 us)
Async XLA Ops:
  7.2 6.5 %copy-start = (bf16[128,1536]{1,0:T(8,128)(2,1)S(1)}, bf16[128,1536]{1,0:T(8,128)(2,1)}, u32[]{:S(2)}) copy-start(bf16[128,1536]{1,0:T(8,128)(2,1)} %param.10) | copy-start | bytes 1179652
  7.2 178.9 %all-gather.5.cloned.1.call-start = ((), (), s32[]{:S(2)}) async-start(), calls=%async_computation.5 | async-start | bytes 9830400 | tf_op jit(solution)/shard_map/all_gather | solution.py:81
  58.7 4.3 %copy-start.4 = (f32[128,1536]{1,0:T(8,128)S(1)}, f32[128,1536]{1,0:T(8,128)}, u32[]{:S(2)}) copy-start(f32[128,1536]{1,0:T(8,128)} %param.9) | copy-start | bytes 2359300
  62.8 157.5 %all-gather.3.cloned.1.call-start = ((), (), s32[]{:S(2)}) async-start(), calls=%async_computation.4 | async-start | bytes 9830400 | tf_op jit(solution)/shard_map/all_gather | solution.py:83
  102.6 4.2 %copy-start.2 = (bf16[640,1536]{1,0:T(8,128)(2,1)S(1)}, bf16[640,1536]{1,0:T(8,128)(2,1)}, u32[]{:S(2)}) copy-start(bf16[640,1536]{1,0:T(8,128)(2,1)} %reshape.95) | copy-start | bytes 5898244
  106.8 12.0 %slice-start.2 = ((s8[4718592]{0:T(1024)(128)(4,1)}), s8[4194304]{0:T(1024)(128)(4,1)S(1)}, s32[]{:S(2)}) async-start(s8[4718592]{0:T(1024)(128)(4,1)} %bitcast.63), calls=%async_computation.8 | async-start | bytes 8388608
  112.1 6.7 %copy-start.11 = (f32[640,1536]{1,0:T(8,128)}, f32[640,1536]{1,0:T(8,128)S(1)}, u32[]{:S(2)}) copy-start(f32[640,1536]{1,0:T(8,128)S(1)} %fusion.6) | copy-start | bytes 11796484
  112.1 6.7 %copy-start.3 = (bf16[640,1536]{1,0:T(8,128)(2,1)S(1)}, bf16[640,1536]{1,0:T(8,128)(2,1)}, u32[]{:S(2)}) copy-start(bf16[640,1536]{1,0:T(8,128)(2,1)} %reshape.93) | copy-start | bytes 5898244
  112.1 6.7 %slice-start.3 = ((s8[4718592]{0:T(1024)(128)(4,1)}), s8[524288]{0:T(1024)(128)(4,1)S(1)}, s32[]{:S(2)}) async-start(s8[4718592]{0:T(1024)(128)(4,1)} %bitcast.63), calls=%async_computation.9 | async-start | bytes 1048576
  118.8 5.4 %copy-start.9 = (f32[640,1536]{1,0:T(8,128)}, f32[640,1536]{1,0:T(8,128)S(1)}, u32[]{:S(2)}) copy-start(f32[640,1536]{1,0:T(8,128)S(1)} %fusion.2) | copy-start | bytes 11796484
  124.9 20.7 %all-to-all-start.3 = ((bf16[32,1,20]{2,1,0:T(2,128)(2,1)}), bf16[32,1,20]{2,1,0:T(2,128)(2,1)S(1)}, u32[]{:S(2)}, u32[]{:S(2)}) async-start(bf16[32,1,20]{2,1,0:T(2,128)(2,1)} %convert_element_type.97), calls=%async_computation.3 | async-start | bytes 32768 | tf_op jit(solution)/shard_map/all_to_all | solution.py:78
  128.8 9.0 %copy-start.10 = (f32[640,1536]{1,0:T(8,128)S(1)}, f32[640,1536]{1,0:T(8,128)}, u32[]{:S(2)}) copy-start(f32[640,1536]{1,0:T(8,128)} %copy-done.9) | copy-start | bytes 11796484
  128.8 9.0 %copy-start.13 = (f32[640,1536]{1,0:T(8,128)S(1)}, f32[640,1536]{1,0:T(8,128)}, u32[]{:S(2)}) copy-start(f32[640,1536]{1,0:T(8,128)} %get-tuple-element.12) | copy-start | bytes 11796484
  143.6 9.8 %copy-start.5 = (f32[128,4]{0,1:T(4,128)S(1)}, f32[128,4]{0,1:T(4,128)}, u32[]{:S(2)}) copy-start(f32[128,4]{0,1:T(4,128)} %param.11) | copy-start | bytes 6148
  145.7 38.9 %all-to-all-start.2 = ((bf16[32,20,1536]{2,1,0:T(8,128)(2,1)}), bf16[32,20,1536]{2,1,0:T(8,128)(2,1)S(1)}, u32[]{:S(2)}, u32[]{:S(2)}) async-start(bf16[32,20,1536]{2,1,0:T(8,128)(2,1)} %reshape.96), calls=%async_computation.2 | async-start | bytes 4718592 | tf_op jit(solution)/shard_map/all_to_all | solution.py:78
  186.1 9.9 %copy-start.6 = (bf16[2560,1536]{1,0:T(8,128)(2,1)S(1)}, bf16[2560,1536]{1,0:T(8,128)(2,1)}, u32[]{:S(2)}) copy-start(bf16[2560,1536]{1,0:T(8,128)(2,1)} %all-gather.5.cloned.1.call-done) | copy-start | bytes 23592964
  220.3 7.4 %copy-start.7 = (bf16[2560,1536]{1,0:T(8,128)(2,1)S(1)}, bf16[2560,1536]{1,0:T(8,128)(2,1)}, u32[]{:S(2)}) copy-start(bf16[2560,1536]{1,0:T(8,128)(2,1)} %all-gather.5.cloned.1.call-done) | copy-start | bytes 23592964
  220.3 7.4 %copy-start.8 = (f32[2560,384]{1,0:T(8,128)S(1)}, f32[2560,384]{1,0:T(8,128)}, u32[]{:S(2)}) copy-start(f32[2560,384]{1,0:T(8,128)} %fusion.25) | copy-start | bytes 11796484
  227.7 4.5 %copy-start.12 = (f32[2560,384]{1,0:T(8,128)S(1)}, f32[2560,384]{1,0:T(8,128)}, u32[]{:S(2)}) copy-start(f32[2560,384]{1,0:T(8,128)} %convolution_add_fusion) | copy-start | bytes 11796484
  227.7 9.0 %slice-start = ((s8[7864320]{0:T(1024)(128)(4,1)}), s8[4194304]{0:T(1024)(128)(4,1)S(1)}, s32[]{:S(2)}) async-start(s8[7864320]{0:T(1024)(128)(4,1)} %bitcast.61), calls=%async_computation.6 | async-start | bytes 8388608
  232.2 4.6 %slice-start.1 = ((s8[7864320]{0:T(1024)(128)(4,1)}), s8[3670016]{0:T(1024)(128)(4,1)S(1)}, s32[]{:S(2)}) async-start(s8[7864320]{0:T(1024)(128)(4,1)} %bitcast.61), calls=%async_computation.7 | async-start | bytes 7340032
  236.7 4.4 %copy-start.1 = (bf16[128,1536]{1,0:T(8,128)(2,1)S(1)}, bf16[128,1536]{1,0:T(8,128)(2,1)}, u32[]{:S(2)}) copy-start(bf16[128,1536]{1,0:T(8,128)(2,1)} %param.10) | copy-start | bytes 1179652
Sparse Core Ops, SparseCore 0:
  62.9 76.0 all-gather.4
  140.7 79.5 all-gather.2
where the time goes:
time: 249 us; the launch traced here: 248 us
  matrix products  76.9 us (31%)
  blocking collectives  75.7 us (30%)
  waiting for transfers between devices  47.5 us (19%)
  local copies, waits for them, and re-layouts  16.4 us (7%)
  between operations  14.4 us (6%)
  starting transfers between devices  11.2 us (4%)
  other arithmetic  5.9 us (2%)
    all_to_all x2, blocking collectives, exchange(): return lax.all_to_all(a, 'ep', split_axis=0, concat_axis=0, tiled=True)  75.7 us
    dot_general x6, matrix products, contract_last(): lax.dot_general(first_op, second_op, (((1,), (1,)), ((), ())), preferred_...  42 us
    all_to_all x2, waiting for transfers between devices, exchange(): return lax.all_to_all(a, 'ep', split_axis=0, concat_axis=0, tiled=True)  30.6 us
    all_gather x1, waiting for transfers between devices, on_device(): all_g = lax.all_gather(slot_g, 'dp', axis=0, tiled=True)  16.9 us
    dot_general x3, matrix products, contract_first(): lax.dot_general(first_op, second_op, (((0,), (0,)), ((), ())), preferred_...  13.4 us
    all_to_all x2, starting transfers between devices, exchange(): return lax.all_to_all(a, 'ep', split_axis=0, concat_axis=0, tiled=True)  11.1 us
    dot_general x1, matrix products, on_device(): jnp.dot(gate_delta, w_gate, preferred_element_type=jnp.float32)  8.95 us
    dot_general x1, matrix products, on_device(): jnp.dot(up_delta, w_up, preferred_element_type=jnp.float32)  5.8 us
  transfers between devices with their start and end apart: 4, of which 2 were waited for; matrix products, arithmetic and copies ran while one was open for 26% of the time, Pallas kernels for 0%

commit v1 on v0

--- a/solution.py
+++ b/solution.py
@@ -1,9 +1,20 @@
+import functools
 import jax
 import jax.numpy as jnp
 from jax import lax
 from jax.sharding import PartitionSpec as P
 
 sharpness = 1.702
+
+
+def set_task_now(packet, row_axis):
+    return jnp.concatenate(
+        lax.all_to_all(jnp.stack([packet for _ in range(lax.axis_size(row_axis))]), row_axis, 0, 0),
+        axis=0,
+    )
+
+
+rates_replace = functools.partial(set_task_now, row_axis="dp")
 
 
 def contract_last(first_op, second_op):
@@ -80,7 +91,7 @@
     slot_x = exchange(send_x.reshape(bucket_shape)).reshape(slot_rows, model_width)
     all_x = lax.all_gather(slot_x, "dp", axis=0, tiled=True)
     slot_g = exchange(send_g.reshape(bucket_shape)).reshape(slot_rows, model_width)
-    all_g = lax.all_gather(slot_g, "dp", axis=0, tiled=True)
+    all_g = rates_replace(slot_g)
     w_gate = gate_weight[0]
     w_up = up_weight[0]
     w_down = down_weight[0]

time: 249 us -> 318 us (1.28)
  waiting for transfers between devices: 47.5 us -> 126 us
  blocking collectives: 75.7 us -> 38.9 us
  starting transfers between devices: 11.2 us -> 27.2 us
  matrix products: 76.9 us -> 86.8 us
    all_to_all x0 -> x1, waiting for transfers between devices: none -> 85.7 us  [set_task_now(): lax.all_to_all(jnp.stack([packet for _ in range(lax.axis_size(row_axis))]...]
    all_to_all x2 -> x1, blocking collectives: 75.7 us -> 38.9 us  [exchange(): return lax.all_to_all(a, 'ep', split_axis=0, concat_axis=0, tiled=True)]
    all_gather x1 -> x0, waiting for transfers between devices: 16.9 us -> none  [on_device(): all_g = lax.all_gather(slot_g, 'dp', axis=0, tiled=True)]
    all_to_all x2 -> x3, starting transfers between devices: 11.1 us -> 21.4 us  [exchange(): return lax.all_to_all(a, 'ep', split_axis=0, concat_axis=0, tiled=True)]
    all_to_all x2 -> x3, waiting for transfers between devices: 30.6 us -> 39.9 us  [exchange(): return lax.all_to_all(a, 'ep', split_axis=0, concat_axis=0, tiled=True)]
    all_to_all x0 -> x1, starting transfers between devices: none -> 5.74 us  [set_task_now(): lax.all_to_all(jnp.stack([packet for _ in range(lax.axis_size(row_axis))]...]
    dot_general x6, matrix products: 42 us -> 47.3 us  [contract_last(): lax.dot_general(first_op, second_op, (((1,), (1,)), ((), ())), preferred_...]
    another operation x0 -> x1, local copies, waits for them, and re-layouts: none -> 3.73 us  [set_task_now(): jnp.stack([packet for _ in range(lax.axis_size(row_axis))])]
  transfers between devices with their start and end apart: 4 -> 5, of which waited for: 2 -> 3; matrix products, arithmetic and copies ran while one was open for 26% -> 23% of each run, Pallas kernels for 0% -> 0%
where the time goes in v1:
time: 318 us; the launch traced here: 317 us
  waiting for transfers between devices  126 us (40%)
  matrix products  86.8 us (27%)
  blocking collectives  38.9 us (12%)
  starting transfers between devices  27.2 us (9%)
  local copies, waits for them, and re-layouts  18 us (6%)
  between operations  14.3 us (4%)
  other arithmetic  5.91 us (2%)
    all_to_all x1, waiting for transfers between devices, set_task_now(): lax.all_to_all(jnp.stack([packet for _ in range(lax.axis_size(row_axis))]...  85.7 us
    dot_general x6, matrix products, contract_last(): lax.dot_general(first_op, second_op, (((1,), (1,)), ((), ())), preferred_...  47.3 us
    all_to_all x3, waiting for transfers between devices, exchange(): return lax.all_to_all(a, 'ep', split_axis=0, concat_axis=0, tiled=True)  39.9 us
    all_to_all x1, blocking collectives, exchange(): return lax.all_to_all(a, 'ep', split_axis=0, concat_axis=0, tiled=True)  38.9 us
    all_to_all x3, starting transfers between devices, exchange(): return lax.all_to_all(a, 'ep', split_axis=0, concat_axis=0, tiled=True)  21.4 us
    dot_general x3, matrix products, contract_first(): lax.dot_general(first_op, second_op, (((0,), (0,)), ((), ())), preferred_...  16.9 us
    dot_general x1, matrix products, on_device(): jnp.dot(gate_delta, w_gate, preferred_element_type=jnp.float32)  9.07 us
    dot_general x1, matrix products, on_device(): jnp.dot(up_delta, w_up, preferred_element_type=jnp.float32)  7.07 us
  transfers between devices with their start and end apart: 5, of which 3 were waited for; matrix products, arithmetic and copies ran while one was open for 23% of the time, Pallas kernels for 0%

profile of v1, /device:TPU:1, one launch (start us, length us, event | category | flops | bytes accessed | tf_op | source)
XLA Modules:
  0.0 316.6 jit_solution(16123422974308448351)
XLA Ops:
  7.2 0.0 copy-start
  7.2 0.7 convert_element_type.78
  7.9 0.7 fusion.39
  8.6 0.8 select_reduce_fusion
  9.4 0.9 fusion.40
  10.3 0.7 select_reduce_fusion.1
  11.0 1.3 abs_reduce_fusion
  12.3 1.0 fusion.24
  13.3 0.2 multiply_reduce_fusion.2
  13.5 0.1 copy.29
  13.6 0.7 convolution_convert_fusion
  14.2 2.1 reshape.99
  16.3 9.4 %all-to-all-start.1 = ((bf16[32,20,1536]{2,1,0:T(8,128)(2,1)}), bf16[32,20,1536]{2,1,0:T(8,128)(2,1)S(1)}, u32[]{:S(2)}, u32[]{:S(2)}) async-start(bf16[32,20,1536]{2,1,0:T(8,128)(2,1)} %reshape.99), calls=%async_computation.1 | async-start | bytes 4718592 | tf_op jit(solution)/shard_map/all_to_all | solution.py:89
  25.8 0.1 copy.30
  25.9 0.1 mul.136
  26.0 3.2 multiply_convert_fusion.5
  29.1 4.0 %reshape.97 = bf16[32,20,1536]{2,1,0:T(8,128)(2,1)} reshape(bf16[640,1536]{1,0:T(8,128)(2,1)} %multiply_convert_fusion.5) | data formatting | bytes 3932160 | tf_op jit(solution)/shard_map/reshape | solution.py:93
  33.1 24.2 %all-to-all-done.1 = bf16[32,20,1536]{2,1,0:T(8,128)(2,1)S(1)} async-done(((bf16[32,20,1536]{2,1,0:T(8,128)(2,1)}), bf16[32,20,1536]{2,1,0:T(8,128)(2,1)S(1)}, u32[]{:S(2)}, u32[]{:S(2)}) %all-to-all-start.1) | async-done | bytes 1966112 | tf_op jit(solution)/shard_map/all_to_all | solution.py:89
  57.3 6.3 %all-to-all-start = ((bf16[32,20,1536]{2,1,0:T(8,128)(2,1)}), bf16[32,20,1536]{2,1,0:T(8,128)(2,1)}, u32[]{:S(2)}, u32[]{:S(2)}) async-start(bf16[32,20,1536]{2,1,0:T(8,128)(2,1)} %reshape.97), calls=%async_computation | async-start | bytes 4718592 | tf_op jit(solution)/shard_map/all_to_all | solution.py:89
  63.6 0.0 all-gather.2.cloned.1.call-start
  63.6 2.0 reshape.100
  65.6 0.0 all-gather.2.cloned.1.call-update
  65.6 0.0 slice-start.1
  65.6 8.3 %fusion.6 = f32[640,1536]{1,0:T(8,128)} fusion(bf16[640,1536]{1,0:T(8,128)(2,1)} %reshape.100, bf16[1,1536,1536]{2,1,0:T(8,128)(2,1)} %param.16), kind=kOutput, calls=%fused_computation.6 | convolution fusion | flops 3019898880 | bytes 10616832 | tf_op jit(solution)/shard_map/dot_general | solution.py:21
  73.9 5.2 %fusion.2 = f32[640,1536]{1,0:T(8,128)} fusion(bf16[640,1536]{1,0:T(8,128)(2,1)S(1)} %copy-done.5, bf16[1,1536,1536]{2,1,0:T(8,128)(2,1)S(1)} %bitcast.63), kind=kOutput, calls=%fused_computation.2 | convolution fusion | flops 3019898880 | bytes 10616832 | tf_op jit(solution)/shard_map/dot_general | solution.py:21
  79.1 15.7 %all-to-all-done = bf16[32,20,1536]{2,1,0:T(8,128)(2,1)} async-done(((bf16[32,20,1536]{2,1,0:T(8,128)(2,1)}), bf16[32,20,1536]{2,1,0:T(8,128)(2,1)}, u32[]{:S(2)}, u32[]{:S(2)}) %all-to-all-start) | async-done | bytes 1966112 | tf_op jit(solution)/shard_map/all_to_all | solution.py:89
  94.8 2.6 reshape.98
  97.5 10.8 %multiply_reduce_fusion = (bf16[640]{0:T(1024)(128)(2,1)S(1)}, f32[640,1536]{1,0:T(8,128)}) fusion(f32[640,1536]{1,0:T(8,128)} %fusion.6, f32[640,1536]{1,0:T(8,128)} %fusion.2, bf16[640,1536]{1,0:T(8,128)(2,1)S(1)} %reshape.98, bf16[1,1536,1536]{2,1,0:T(8,128)(2,1)} %param.17), kind=kOutput, calls=%fused_computation.15 | convolution fusion | flops 3028745728 | bytes 18482432 | tf_op jit(solution)/shard_map/dot_general | solution.py:21
  108.3 0.7 convert_element_type.97
  109.0 5.7 %all-to-all-start.3 = ((bf16[32,1,20]{2,1,0:T(2,128)(2,1)}), bf16[32,1,20]{2,1,0:T(2,128)(2,1)S(1)}, u32[]{:S(2)}, u32[]{:S(2)}) async-start(bf16[32,1,20]{2,1,0:T(2,128)(2,1)} %convert_element_type.97), calls=%async_computation.3 | async-start | bytes 32768 | tf_op jit(solution)/shard_map/all_to_all | solution.py:89
  114.7 9.1 %fusion = f32[640,1536]{1,0:T(8,128)S(1)} fusion(bf16[1,1536,1536]{2,1,0:T(8,128)(2,1)} %param.15, f32[640,1536]{1,0:T(8,128)} %get-tuple-element.12, f32[640,1536]{1,0:T(8,128)} %fusion.2, f32[640,1536]{1,0:T(8,128)} %fusion.6), kind=kOutput, calls=%fused_computation | convolution fusion | flops 3031695360 | bytes 20447232 | tf_op jit(solution)/shard_map/dot_general | solution.py:100
  123.8 7.1 %add_convert_fusion = bf16[640,1536]{1,0:T(8,128)(2,1)} fusion(f32[640,1536]{1,0:T(8,128)S(1)} %fusion, bf16[1,1536,1536]{2,1,0:T(8,128)(2,1)} %param.16, f32[640,1536]{1,0:T(8,128)S(1)} %copy-done.10, f32[640,1536]{1,0:T(8,128)S(1)} %copy-done.9), kind=kOutput, calls=%fused_computation.16 | convolution fusion | flops 3028746240 | bytes 18481152 | tf_op jit(solution)/shard_map/dot_general | solution.py:101
  130.9 2.5 reshape.101
  133.4 0.0 all-to-all-done.3
  133.4 38.9 %all_to_all.29 = bf16[32,20,1536]{2,1,0:T(8,128)(2,1)} all-to-all(bf16[32,20,1536]{2,1,0:T(8,128)(2,1)S(1)} %reshape.101), channel_id=1, replica_groups=mesh['ep'=32,'dp'=4] {'ep'}, dimensions={0} | all-to-all | bytes 3932160 | tf_op jit(solution)/shard_map/all_to_all | solution.py:89
  172.3 3.7 %stack.3 = bf16[4,640,1536]{2,1,0:T(8,128)(2,1)} broadcast(bf16[640,1536]{1,0:T(8,128)(2,1)S(1)} %copy-done.4), dimensions={1,2} | broadcast | bytes 9830400 | tf_op jit(solution)/shard_map/stack | solution.py:12
  176.0 5.7 %all-to-all-start.4 = ((bf16[4,640,1536]{2,1,0:T(8,128)(2,1)}), bf16[4,640,1536]{2,1,0:T(8,128)(2,1)}, u32[]{:S(2)}, u32[]{:S(2)}) async-start(bf16[4,640,1536]{2,1,0:T(8,128)(2,1)} %stack.3), calls=%async_computation.4 | async-start | bytes 15728640 | tf_op jit(solution)/shard_map/all_to_all | solution.py:12
  181.8 0.1 copy.33
  181.9 0.2 fusion.17
  182.1 0.6 div.20
  182.7 1.5 fusion.19
  184.3 85.7 %all-to-all-done.4 = bf16[4,640,1536]{2,1,0:T(8,128)(2,1)} async-done(((bf16[4,640,1536]{2,1,0:T(8,128)(2,1)}), bf16[4,640,1536]{2,1,0:T(8,128)(2,1)}, u32[]{:S(2)}, u32[]{:S(2)}) %all-to-all-start.4) | async-done | bytes 7864352 | tf_op jit(solution)/shard_map/all_to_all | solution.py:12
  269.9 9.7 %fusion.28 = f32[2560,384]{1,0:T(8,128)} fusion(bf16[2560,1536]{1,0:T(8,128)(2,1)} %bitcast.8, bf16[1,1536,1536]{2,1,0:T(8,128)(2,1)} %param.17, s32[]{:T(128)S(6)} %select_n.2), kind=kOutput, calls=%fused_computation.44 | convolution fusion | flops 3019898880 | bytes 12976132 | tf_op jit(solution)/shard_map/dot_general | solution.py:21
  279.6 7.7 %convolution_add_fusion = f32[2560,384]{1,0:T(8,128)S(1)} fusion(bf16[2560,1536]{1,0:T(8,128)(2,1)} %all-gather.2.cloned.1.call-done, bf16[1,1536,1536]{2,1,0:T(8,128)(2,1)} %param.16, s32[]{:T(128)S(6)} %select_n.2), kind=kOutput, calls=%fused_computation.10 | convolution fusion | flops 3020881920 | bytes 12976132 | tf_op jit(solution)/shard_map/dot_general | solution.py:21
  287.3 5.6 %fusion.25 = f32[2560,384]{1,0:T(8,128)S(1)} fusion(bf16[2560,1536]{1,0:T(8,128)(2,1)S(1)} %copy-done.7, bf16[1,1536,1536]{2,1,0:T(8,128)(2,1)} %param.15, s32[]{:T(128)S(6)} %select_n.2), kind=kOutput, calls=%fused_computation.41 | convolution fusion | flops 3019898880 | bytes 12976132 | tf_op jit(solution)/shard_map/dot_general | solution.py:21
  292.9 7.9 %fusion.16 = bf16[1,384,1536]{2,1,0:T(8,128)(2,1)} fusion(bf16[2560,1536]{1,0:T(8,128)(2,1)} %bitcast.8, f32[2560,384]{1,0:T(8,128)S(1)} %convolution_add_fusion, f32[2560,384]{1,0:T(8,128)S(1)} %fusion.25), kind=kOutput, calls=%fused_computation.29 | convolution fusion | flops 3027369984 | bytes 16908288 | tf_op jit(solution)/shard_map/dot_general | solution.py:27
  300.8 4.5 %fusion.14 = bf16[1,384,1536]{2,1,0:T(8,128)(2,1)} fusion(bf16[2560,1536]{1,0:T(8,128)(2,1)S(1)} %copy-done.7, f32[2560,384]{1,0:T(8,128)S(1)} %copy-done.8, f32[2560,384]{1,0:T(8,128)S(1)} %convolution_add_fusion, f32[2560,384]{1,0:T(8,128)S(1)} %fusion.25), kind=kOutput, calls=%fused_computation.27 | convolution fusion | flops 3031302144 | bytes 20840448 | tf_op jit(solution)/shard_map/dot_general | solution.py:27
  305.4 4.4 %fusion.15 = bf16[1,384,1536]{2,1,0:T(8,128)(2,1)} fusion(bf16[2560,1536]{1,0:T(8,128)(2,1)S(1)} %copy-done.7, f32[2560,384]{1,0:T(8,128)S(1)} %copy-done.8, f32[2560,384]{1,0:T(8,128)S(1)} %fusion.25), kind=kOutput, calls=%fused_computation.28 | convolution fusion | flops 3027369984 | bytes 16908288 | tf_op jit(solution)/shard_map/dot_general | solution.py:27
  (31 shorter events, 0.1 us)
Async XLA Ops:
  7.2 6.4 %copy-start = (bf16[128,1536]{1,0:T(8,128)(2,1)S(1)}, bf16[128,1536]{1,0:T(8,128)(2,1)}, u32[]{:S(2)}) copy-start(bf16[128,1536]{1,0:T(8,128)(2,1)} %param.10) | copy-start | bytes 1179652
  16.3 40.9 %all-to-all-start.1 = ((bf16[32,20,1536]{2,1,0:T(8,128)(2,1)}), bf16[32,20,1536]{2,1,0:T(8,128)(2,1)S(1)}, u32[]{:S(2)}, u32[]{:S(2)}) async-start(bf16[32,20,1536]{2,1,0:T(8,128)(2,1)} %reshape.99), calls=%async_computation.1 | async-start | bytes 4718592 | tf_op jit(solution)/shard_map/all_to_all | solution.py:89
  57.3 37.6 %all-to-all-start = ((bf16[32,20,1536]{2,1,0:T(8,128)(2,1)}), bf16[32,20,1536]{2,1,0:T(8,128)(2,1)}, u32[]{:S(2)}, u32[]{:S(2)}) async-start(bf16[32,20,1536]{2,1,0:T(8,128)(2,1)} %reshape.97), calls=%async_computation | async-start | bytes 4718592 | tf_op jit(solution)/shard_map/all_to_all | solution.py:89
  63.6 216.0 %all-gather.2.cloned.1.call-start = ((), (), s32[]{:S(2)}) async-start(), calls=%async_computation.5 | async-start | bytes 9830400 | tf_op jit(solution)/shard_map/all_gather | solution.py:92
  65.6 8.3 %slice-start = ((s8[4718592]{0:T(1024)(128)(4,1)}), s8[524288]{0:T(1024)(128)(4,1)S(1)}, s32[]{:S(2)}) async-start(s8[4718592]{0:T(1024)(128)(4,1)} %bitcast.62), calls=%async_computation.6 | async-start | bytes 1048576
  65.6 8.3 %copy-start.5 = (bf16[640,1536]{1,0:T(8,128)(2,1)S(1)}, bf16[640,1536]{1,0:T(8,128)(2,1)}, u32[]{:S(2)}) copy-start(bf16[640,1536]{1,0:T(8,128)(2,1)} %reshape.100) | copy-start | bytes 5898244
  65.6 8.3 %slice-start.1 = ((s8[4718592]{0:T(1024)(128)(4,1)}), s8[4194304]{0:T(1024)(128)(4,1)S(1)}, s32[]{:S(2)}) async-start(s8[4718592]{0:T(1024)(128)(4,1)} %bitcast.62), calls=%async_computation.7 | async-start | bytes 8388608
  97.4 10.9 %copy-start.3 = (bf16[640,1536]{1,0:T(8,128)(2,1)}, bf16[640,1536]{1,0:T(8,128)(2,1)S(1)}, u32[]{:S(2)}) copy-start(bf16[640,1536]{1,0:T(8,128)(2,1)S(1)} %reshape.98) | copy-start | bytes 5898244
  109.0 24.3 %all-to-all-start.3 = ((bf16[32,1,20]{2,1,0:T(2,128)(2,1)}), bf16[32,1,20]{2,1,0:T(2,128)(2,1)S(1)}, u32[]{:S(2)}, u32[]{:S(2)}) async-start(bf16[32,1,20]{2,1,0:T(2,128)(2,1)} %convert_element_type.97), calls=%async_computation.3 | async-start | bytes 32768 | tf_op jit(solution)/shard_map/all_to_all | solution.py:89
  114.7 9.1 %copy-start.9 = (f32[640,1536]{1,0:T(8,128)S(1)}, f32[640,1536]{1,0:T(8,128)}, u32[]{:S(2)}) copy-start(f32[640,1536]{1,0:T(8,128)} %fusion.2) | copy-start | bytes 11796484
  114.7 9.1 %copy-start.10 = (f32[640,1536]{1,0:T(8,128)S(1)}, f32[640,1536]{1,0:T(8,128)}, u32[]{:S(2)}) copy-start(f32[640,1536]{1,0:T(8,128)} %get-tuple-element.12) | copy-start | bytes 11796484
  133.4 38.9 %copy-start.4 = (bf16[640,1536]{1,0:T(8,128)(2,1)S(1)}, bf16[640,1536]{1,0:T(8,128)(2,1)}, u32[]{:S(2)}) copy-start(bf16[640,1536]{1,0:T(8,128)(2,1)} %copy-done.3) | copy-start | bytes 5898244
  176.0 6.1 %copy-start.6 = (f32[128,4]{0,1:T(4,128)S(1)}, f32[128,4]{0,1:T(4,128)}, u32[]{:S(2)}) copy-start(f32[128,4]{0,1:T(4,128)} %param.11) | copy-start | bytes 6148
  176.0 6.7 %copy-start.2 = (bf16[32,20,1536]{2,1,0:T(8,128)(2,1)S(1)}, bf16[32,20,1536]{2,1,0:T(8,128)(2,1)}, u32[]{:S(2)}) copy-start(bf16[32,20,1536]{2,1,0:T(8,128)(2,1)} %all_to_all.29) | copy-start | bytes 5898244
  176.0 93.9 %all-to-all-start.4 = ((bf16[4,640,1536]{2,1,0:T(8,128)(2,1)}), bf16[4,640,1536]{2,1,0:T(8,128)(2,1)}, u32[]{:S(2)}, u32[]{:S(2)}) async-start(bf16[4,640,1536]{2,1,0:T(8,128)(2,1)} %stack.3), calls=%async_computation.4 | async-start | bytes 15728640 | tf_op jit(solution)/shard_map/all_to_all | solution.py:12
  279.6 7.7 %copy-start.7 = (bf16[2560,1536]{1,0:T(8,128)(2,1)S(1)}, bf16[2560,1536]{1,0:T(8,128)(2,1)}, u32[]{:S(2)}) copy-start(bf16[2560,1536]{1,0:T(8,128)(2,1)} %all-gather.2.cloned.1.call-done) | copy-start | bytes 23592964
  292.9 7.9 %copy-start.8 = (f32[2560,384]{1,0:T(8,128)S(1)}, f32[2560,384]{1,0:T(8,128)}, u32[]{:S(2)}) copy-start(f32[2560,384]{1,0:T(8,128)} %fusion.28) | copy-start | bytes 11796484
  305.4 4.4 %copy-start.1 = (bf16[128,1536]{1,0:T(8,128)(2,1)S(1)}, bf16[128,1536]{1,0:T(8,128)(2,1)}, u32[]{:S(2)}) copy-start(bf16[128,1536]{1,0:T(8,128)(2,1)} %param.10) | copy-start | bytes 1179652
Sparse Core Ops, SparseCore 0:
  66.0 79.8 all-gather.1
